TPU v7x, 256 devices: a whole 4x4x8 slice. The times are simulated.
256 devices in a mesh: section: 8 (over z), ctx: 32 (over x, y, core).
Axes of the slice: x: 4, y: 4, z: 8, core: 2. Of those that a mesh axis runs over, the one named last changes fastest.
Arguments:
- queries: bfloat16 [8, 8192, 3072], P('section', 'ctx'), may hold values from -160 to 160
- keys: bfloat16 [8, 8192, 512], P('section', 'ctx'), may hold values from -48 to 48
- values: bfloat16 [8, 8192, 512], P('section', 'ctx'), may hold values from -15 to 15
- cotangent: bfloat16 [8, 8192, 3072], P('section', 'ctx'), may hold values from -6 to 6
- router_logits: bfloat16 [8, 8192], P('section', 'ctx'), may hold values from -8 to 8
- positions: int32 [8, 8192], P('section', 'ctx'), may hold values from -1 to 32767, as said below
- counts: int32 [8, 32], P('section', 'ctx'), may hold values from 0 to 2, as said below
Outputs:
- handed: bfloat16 [8, 8192, 3072], P('section', 'ctx')
- value_grad: bfloat16 [8, 8192, 512], P('section', 'ctx')
- gate_grad: bfloat16 [8, 8192], P('section', 'ctx')
Inputs may be any that keep to these rules, and one draw needn't show every extreme that they name: For every micro-batch and every shard c, the counts of shards 0 to c sum to c + 1 or c + 2; shard 0 holds 2 blocks; all counts of a micro-batch sum to 32. In shard c's slots, the first counts * 128 hold distinct positions in increasing order, all within c * 1024 to (c + 1) * 1024 - 1; the other slots hold -1.
All inputs are finite; a program needn't handle non-finite values.
Results may differ from a plain program's by a relative error of at most 0.0066.
Values may be sent and summed in bfloat16 or wider, within the bound.
A program may use at most 128 MiB of HBM per device.

v0:
```python
import math
import jax
import jax.numpy as jnp
from jax import lax
from jax.sharding import PartitionSpec as P

QUERY_HEADS = 24
KEY_VALUE_HEADS = 4
HEAD_SIZE = 128
BLOCK_ROWS = 128
MAXB = 2
score_masked_out = -1e30


def copy_for_each(x, axis):
    copies = jnp.broadcast_to(x, (lax.axis_size(axis), *x.shape))
    return lax.all_to_all(copies, axis, split_axis=0, concat_axis=0, tiled=True)


def folded_in_pairs(pieces, combine):
    while len(jax.tree.leaves(pieces)[0]) > 1:
        pieces = jax.vmap(combine)(*(pieces[side::2] for side in (0, 1)))
    return pieces[0]


def carried_in(x, axis, combine, identity):
    devices, mine = (lax.axis_size(axis), lax.axis_index(axis))
    passed = jnp.arange(devices) < mine

    def kept(part, zero, own):
        part = jnp.where(
            passed.reshape(-1, *(1 for _ in own.shape)), part, jnp.asarray(zero, own.dtype)
        )
        return part

    pieces = copy_for_each(x, axis)
    return folded_in_pairs(kept(pieces, identity, x), combine)


def passed_along(block, axis, distance):
    devices = range(lax.axis_size(axis))
    route = [(i - distance, i) for i in devices if i - distance in devices]
    return lax.ppermute(block, axis, route)


def sent_together(arrays, axis, dim, along):
    widths = [a.shape[along] for a in arrays]
    both = jnp.concatenate(arrays, axis=along)
    out = lax.all_gather(both, axis, axis=dim, tiled=True)
    return tuple(jnp.split(out, [sum(widths[:k]) for k in range(1, len(widths))], axis=along))


def for_sending(x):

    def short(part):
        return part.astype(jnp.bfloat16) if part.dtype == jnp.float32 else part

    return jax.tree.map(short, x)


def in_blocks(x, dim, devices):
    before, after = (x.shape[:dim], x.shape[dim + 1 :])
    return jnp.moveaxis(x.reshape(*before, devices, -1, *after), dim, 0)


def sent_and_summed(x, axis, dim):
    devices = lax.axis_size(axis)
    tiles = lax.all_to_all(in_blocks(x, dim, devices), axis, 0, 0, tiled=True)
    return jnp.sum(tiles.astype(jnp.float32), axis=0)


def from_behind(x, axis, by):
    devices = lax.axis_size(axis)
    return lax.ppermute(x, axis, [(i, (i + by) % devices) for i in range(devices)])


def add_ints(earlier, later):
    return earlier + later


def local(queries, keys, values, cotangent, router_logits, positions, counts):
    query_group_width = QUERY_HEADS // KEY_VALUE_HEADS
    shards = lax.axis_size("ctx")
    key_width = BLOCK_ROWS * min(shards, max(1, 512 // BLOCK_ROWS))
    score_scale = 1.0 / math.sqrt(HEAD_SIZE)
    blocks_held = counts[0, 0]
    before = carried_in(blocks_held - 1, "ctx", add_ints, jnp.int32(0))
    carried = before + blocks_held - 1
    last_block = jnp.maximum(blocks_held - 1, 0)
    own_arrays = (queries[0], keys[0], values[0], cotangent[0], router_logits[0], positions[0])
    outgoing = [
        lax.dynamic_slice_in_dim(source, last_block * BLOCK_ROWS, BLOCK_ROWS, 0)
        for source in own_arrays
    ]
    incoming = passed_along(
        (outgoing[0], outgoing[1], outgoing[2], outgoing[3], outgoing[4], outgoing[5]), "ctx", 1
    )
    received_one = before == 1
    chosen = [
        jnp.where(received_one, arriving, source[:BLOCK_ROWS])
        for arriving, source in zip(incoming, own_arrays)
    ]
    query_row_block, key_row_block, value_rows, grad_rows, logit_rows, place_rows = chosen
    gate_values = jax.nn.sigmoid(logit_rows.astype(jnp.float32))
    query_head_rows = query_row_block.reshape(
        BLOCK_ROWS, KEY_VALUE_HEADS, query_group_width, HEAD_SIZE
    )
    latest_query = jnp.max(place_rows)

    def split_width():
        return key_width

    def scores_for(key_portion, place_part):
        local_row_count = key_portion.shape[0]
        scores = (
            jnp.einsum(
                "qhgd,khd->hgqk",
                query_head_rows,
                key_portion.reshape(local_row_count, KEY_VALUE_HEADS, HEAD_SIZE),
                preferred_element_type=jnp.float32,
            )
            * score_scale
        )
        allowed = place_part[None, :] <= place_rows[:, None]
        return (scores, allowed)

    def absorb_part(running, key_portion, value_portion, place_part):
        row_top, weight_sum, summed = running
        local_row_count = key_portion.shape[0]
        scores, allowed = scores_for(key_portion, place_part)
        new_top = jnp.maximum(
            row_top, jnp.max(jnp.where(allowed, scores, score_masked_out), axis=-1)
        )
        weights = jnp.where(allowed, jnp.exp(scores - new_top[..., None]), 0.0)
        factor = jnp.exp(row_top - new_top)
        weight_sum = weight_sum * factor + jnp.sum(weights, axis=-1)
        summed = summed * factor[..., None] + jnp.einsum(
            "hgqk,khd->hgqd",
            weights.astype(jnp.bfloat16),
            value_portion.reshape(local_row_count, KEY_VALUE_HEADS, HEAD_SIZE),
            preferred_element_type=jnp.float32,
        )
        return (new_top, weight_sum, summed)

    def absorb(running, key_portion, value_portion, place_part):
        return lax.cond(
            jnp.min(place_part) > latest_query,
            lambda: running,
            lambda: absorb_part(running, key_portion, value_portion, place_part),
        )

    start_state = (
        jnp.full((KEY_VALUE_HEADS, query_group_width, BLOCK_ROWS), score_masked_out, jnp.float32),
        jnp.zeros((KEY_VALUE_HEADS, query_group_width, BLOCK_ROWS), jnp.float32),
        jnp.zeros((KEY_VALUE_HEADS, query_group_width, BLOCK_ROWS, HEAD_SIZE), jnp.float32),
    )
    collected_rows = (
        *sent_together((key_row_block, value_rows), "ctx", 0, 1),
        lax.all_gather(for_sending(place_rows), "ctx", axis=0, tiled=True).astype(place_rows.dtype),
    )
    key_complete = collected_rows[0]
    local_row_count = key_complete.shape[0]
    rows_per_step = split_width()
    relay_step_count = local_row_count // rows_per_step
    stacked = (
        key_complete.reshape(relay_step_count, rows_per_step, KEY_VALUE_HEADS * HEAD_SIZE),
        collected_rows[1].reshape(relay_step_count, rows_per_step, KEY_VALUE_HEADS * HEAD_SIZE),
        collected_rows[2].reshape(relay_step_count, rows_per_step),
    )

    def visit(state_in, member):
        return (absorb(state_in, member[0], member[1], member[2]), None)

    final_state = lax.scan(visit, start_state, stacked)[0]
    row_top, weight_sum, summed = final_state
    attended = jnp.transpose(summed / weight_sum[..., None], (2, 0, 1, 3)).reshape(
        BLOCK_ROWS, QUERY_HEADS * HEAD_SIZE
    )
    log_total = row_top + jnp.log(weight_sum)
    gradient_broad = grad_rows.astype(jnp.float32)
    output_gradient = (
        (gate_values[:, None] * gradient_broad)
        .astype(jnp.bfloat16)
        .reshape(BLOCK_ROWS, KEY_VALUE_HEADS, query_group_width, HEAD_SIZE)
    )

    def value_portion(key_portion, place_part):
        local_row_count = key_portion.shape[0]
        scores, allowed = scores_for(key_portion, place_part)
        probabilities = jnp.where(allowed, jnp.exp(scores - log_total[..., None]), 0.0).astype(
            jnp.bfloat16
        )
        return jnp.einsum(
            "hgqk,qhgd->khd", probabilities, output_gradient, preferred_element_type=jnp.float32
        ).reshape(local_row_count, KEY_VALUE_HEADS * HEAD_SIZE)

    def value_block(key_portion, place_part):
        return lax.cond(
            jnp.min(place_part) > latest_query,
            lambda: jnp.zeros((key_portion.shape[0], KEY_VALUE_HEADS * HEAD_SIZE), jnp.float32),
            lambda: value_portion(key_portion, place_part),
        )

    key_portion = collected_rows[0]
    place_part = collected_rows[2]
    local_row_count = key_portion.shape[0]
    rows_per_step = split_width()
    relay_step_count = local_row_count // rows_per_step
    product_terms = lax.map(
        lambda member: value_block(member[0], member[1]),
        (
            key_portion.reshape(relay_step_count, rows_per_step, KEY_VALUE_HEADS * HEAD_SIZE),
            place_part.reshape(relay_step_count, rows_per_step),
        ),
    )
    value_sum = sent_and_summed(
        product_terms.reshape(local_row_count, KEY_VALUE_HEADS * HEAD_SIZE).astype(jnp.bfloat16),
        "ctx",
        0,
    )
    branch = (gate_values[:, None] * attended).astype(jnp.bfloat16)
    gate_term = (
        gate_values * (1.0 - gate_values) * jnp.sum(gradient_broad * attended, axis=1)
    ).astype(jnp.bfloat16)
    value_finished = value_sum.astype(jnp.bfloat16)
    returned = passed_along((branch, value_finished, gate_term), "ctx", -1)
    local_results = (branch, value_finished, gate_term)
    slot_lists = ([], [], [])
    for slot_index in range(MAXB):
        local_slot = jnp.logical_and(before == 0, slot_index == 0)
        back_slot = jnp.logical_and(carried == 1, blocks_held - 1 == slot_index)
        for member_index in range(3):
            mine = local_results[member_index]
            filled = jnp.where(
                local_slot, mine, jnp.where(back_slot, returned[member_index], jnp.zeros_like(mine))
            )
            slot_lists[member_index].append(filled)
    owner_branch = jnp.concatenate(slot_lists[0], axis=0)
    value_grad = jnp.concatenate(slot_lists[1], axis=0)
    gate_grad = jnp.concatenate(slot_lists[2], axis=0)
    handed = from_behind(owner_branch, "section", 1)
    return (handed[None], value_grad[None], gate_grad[None])


def solution(mesh):
    return jax.shard_map(
        local,
        mesh=mesh,
        in_specs=(
            P("section", "ctx", None),
            P("section", "ctx", None),
            P("section", "ctx", None),
            P("section", "ctx", None),
            P("section", "ctx"),
            P("section", "ctx"),
            P("section", "ctx"),
        ),
        out_specs=(P("section", "ctx", None), P("section", "ctx", None), P("section", "ctx")),
        check_vma=False,
    )
```

profile of v0, /device:TPU:2, one launch (start us, length us, event | category | flops | bytes accessed | tf_op | source)
XLA Modules:
  0.0 349.3 jit_solution(6655201932795278297)
XLA Ops:
  8.4 7.6 %all-to-all-start = ((s32[32,1,1]{2,1,0:T(1,128)}), s32[32,1,1]{2,1,0:T(1,128)S(1)}, u32[]{:S(2)}, u32[]{:S(2)}) async-start(s32[32,1,1]{2,1,0:T(1,128)} %broadcast_in_dim.73), calls=%async_computation | async-start | bytes 32768 | tf_op jit(solution)/shard_map/all_to_all | solution.py:17
  20.0 3.4 collective-permute-start.2
  35.4 2.8 collective-permute-start.1
  41.3 3.2 collective-permute-start
  45.3 5.1 %collective-permute-done.1 = s32[128]{0:T(128)S(1)} collective-permute-done((s32[128]{0:T(128)S(1)}, s32[128]{0:T(128)S(1)}, u32[]{:S(2)}, u32[]{:S(2)}) %collective-permute-start.1) | collective-permute-done | bytes 544 | tf_op jit(solution)/shard_map/ppermute | solution.py:43
  51.0 21.7 %all-gather = s32[32,1,128]{2,1,0:T(1,128)S(1)} all-gather(s32[1,1,128]{2,1,0:T(1,128)S(1)} %bitcast.117), channel_id=1, replica_groups=mesh['section'=8,'ctx'=32] {'ctx'}, dimensions={0}, use_global_device_ids=true | all-gather | bytes 16896 | tf_op jit(solution)/shard_map/all_gather | solution.py:159
  75.5 19.5 %all-gather.3.cloned.1.call-done = bf16[4096,1024]{1,0:T(8,128)(2,1)} async-done(((bf16[128,1024]{1,0:T(8,128)(2,1)}), bf16[4096,1024]{1,0:T(8,128)(2,1)}) %all-gather.3.cloned.1.call-update) | async-done | bytes 8388624 | tf_op jit(solution)/shard_map/all_gather | solution.py:49
  95.0 5.8 %fusion.38 = (bf16[4096,512]{1,0:T(8,128)(2,1)}, bf16[4096,512]{1,0:T(8,128)(2,1)}) fusion(bf16[4096,1024]{1,0:T(8,128)(2,1)} %all-gather.3.cloned.1.call-done), kind=kLoop, calls=%fused_computation.78 | loop fusion | bytes 16777216 | tf_op jit(solution)/shard_map/split | solution.py:50
  100.8 6.4 %copy.83 = bf16[8,512,512]{1,2,0:T(8,128)(2,1)} copy(bf16[8,512,512]{2,1,0:T(8,128)(2,1)} %bitcast.106) | data formatting | bytes 8388608 | tf_op jit(solution)/shard_map/while | solution.py:174
  107.2 6.5 %copy.85 = bf16[8,512,512]{1,2,0:T(8,128)(2,1)} copy(bf16[8,512,512]{2,1,0:T(8,128)(2,1)} %bitcast.105) | data formatting | bytes 8388608 | tf_op jit(solution)/shard_map/while | solution.py:174
  113.9 34.6 %while.24 = (s32[]{:T(128)}, f32[4,6,128]{2,1,0:T(8,128)S(1)}, f32[4,6,128]{2,1,0:T(8,128)S(1)}, f32[4,6,128,128]{3,2,1,0:T(8,128)S(1)}, s32[8,512]{1,0:T(8,128)...) while((s32[]{:T(128)}, f32[4,6,128]{2,1,0:T(8,128)S(1)}, ...), condition=%wide.region_7.8_spmd, body=%wide.region_1.7_spmd.sunk | while | flops 823466496 | bytes 26417920 | solution.py:174
  115.9 6.3 %conditional.4 = (f32[4,6,128]{2,1,0:T(8,128)S(1)}, f32[4,6,128]{2,1,0:T(8,128)S(1)}, f32[4,6,128,128]{3,2,1,0:T(8,128)S(1)}) conditional(s32[]{:T(128)} %convert_element_type.71, (s32[1,512]{1,0:T(1,128)S(1)}, s32[128]{0:T(128)S(1)}, bf16[8,512,512]{1,2,0:T(8,128)(2,1)}, s32[]{:T(128)}, bf16[128,4,6,128]{3,0,2,1:T(8,128)(2,1)S(1)}, ...), branch_computations={%region_3.5_spmd, %region_6.6_spmd} | conditional | flops 823465984 | bytes 26389020 | solution.py:146
  124.1 6.3 %conditional.4 = (f32[4,6,128]{2,1,0:T(8,128)S(1)}, f32[4,6,128]{2,1,0:T(8,128)S(1)}, f32[4,6,128,128]{3,2,1,0:T(8,128)S(1)}) conditional(s32[]{:T(128)} %convert_element_type.71, (s32[1,512]{1,0:T(1,128)S(1)}, s32[128]{0:T(128)S(1)}, bf16[8,512,512]{1,2,0:T(8,128)(2,1)}, s32[]{:T(128)}, bf16[128,4,6,128]{3,0,2,1:T(8,128)(2,1)S(1)}, ...), branch_computations={%region_3.5_spmd, %region_6.6_spmd} | conditional | flops 823465984 | bytes 26389020 | solution.py:146
  132.3 6.3 %conditional.4 = (f32[4,6,128]{2,1,0:T(8,128)S(1)}, f32[4,6,128]{2,1,0:T(8,128)S(1)}, f32[4,6,128,128]{3,2,1,0:T(8,128)S(1)}) conditional(s32[]{:T(128)} %convert_element_type.71, (s32[1,512]{1,0:T(1,128)S(1)}, s32[128]{0:T(128)S(1)}, bf16[8,512,512]{1,2,0:T(8,128)(2,1)}, s32[]{:T(128)}, bf16[128,4,6,128]{3,0,2,1:T(8,128)(2,1)S(1)}, ...), branch_computations={%region_3.5_spmd, %region_6.6_spmd} | conditional | flops 823465984 | bytes 26389020 | solution.py:146
  155.1 34.9 %while.25 = (s32[]{:T(128)}, bf16[8,512,512]{2,1,0:T(8,128)(2,1)}, s32[8,512]{1,0:T(8,128)S(1)}, s32[]{:T(128)}, s32[128]{0:T(128)S(1)}, /*index=5*/bf16[8,512,5...) while((s32[]{:T(128)}, bf16[8,512,512]{2,1,0:T(8,128)(2,1)}, ...), condition=%wide.region_12.13_spmd, body=%wide.region_8.12_spmd.sunk | while | flops 811663872 | bytes 5917887 | solution.py:209
  157.0 3.6 %conditional.5 = (bf16[1,512,512]{1,2,0:T(8,128)(2,1)S(1)}) conditional(s32[]{:T(128)} %convert_element_type.72, (s32[1,512]{1,0:T(1,128)S(1)}, s32[128]{0:T(128)S(1)}, bf16[8,512,512]{1,2,0:T(8,128)(2,1)}, s32[]{:T(128)}, bf16[128,4,6,128]{3,0,2,1:T(8,128)(2,1)S(1)}, /*index=5*/f32[4,6,128]{2,1,0:T(8,128)S(1)}, ...), branch_computations={%region_10.10_spmd, %region_11.11_spmd} | conditional | flops 811663360 | bytes 3815948 | solution.py:198
  163.6 3.6 %conditional.5 = (bf16[1,512,512]{1,2,0:T(8,128)(2,1)S(1)}) conditional(s32[]{:T(128)} %convert_element_type.72, (s32[1,512]{1,0:T(1,128)S(1)}, s32[128]{0:T(128)S(1)}, bf16[8,512,512]{1,2,0:T(8,128)(2,1)}, s32[]{:T(128)}, bf16[128,4,6,128]{3,0,2,1:T(8,128)(2,1)S(1)}, /*index=5*/f32[4,6,128]{2,1,0:T(8,128)S(1)}, ...), branch_computations={%region_10.10_spmd, %region_11.11_spmd} | conditional | flops 811663360 | bytes 3815948 | solution.py:198
  170.1 3.6 %conditional.5 = (bf16[1,512,512]{1,2,0:T(8,128)(2,1)S(1)}) conditional(s32[]{:T(128)} %convert_element_type.72, (s32[1,512]{1,0:T(1,128)S(1)}, s32[128]{0:T(128)S(1)}, bf16[8,512,512]{1,2,0:T(8,128)(2,1)}, s32[]{:T(128)}, bf16[128,4,6,128]{3,0,2,1:T(8,128)(2,1)S(1)}, /*index=5*/f32[4,6,128]{2,1,0:T(8,128)S(1)}, ...), branch_computations={%region_10.10_spmd, %region_11.11_spmd} | conditional | flops 811663360 | bytes 3815948 | solution.py:198
  190.0 54.2 %all-to-all-start.1 = ((bf16[32,128,512]{2,1,0:T(8,128)(2,1)}), bf16[32,128,512]{2,1,0:T(8,128)(2,1)}, u32[]{:S(2)}, u32[]{:S(2)}) async-start(bf16[32,128,512]{2,1,0:T(8,128)(2,1)} %bitcast.110), calls=%async_computation.1 | async-start | bytes 8388608 | tf_op jit(solution)/shard_map/all_to_all | solution.py:68
  244.2 4.3 %collective-permute-start.5 = (bf16[128,3072]{0,1:T(8,128)(2,1)S(1)}, bf16[128,3072]{0,1:T(8,128)(2,1)S(1)}, u32[]{:S(2)}, u32[]{:S(2)}) collective-permute-start(bf16[128,3072]{0,1:T(8,128)(2,1)S(1)} %get-tuple-element.429), channel_id=1, source_target_pairs={{1,0},{2,1},{3,2},{4,3},{5,4},{6,5},{7,6},{8,7},{9,8},{10,9},{11,1... | collective-permute-start | bytes 2359304 | tf_op jit(solution)/shard_map/ppermute | solution.py:43
  248.6 53.3 %collective-permute-done.5 = bf16[128,3072]{0,1:T(8,128)(2,1)S(1)} collective-permute-done((bf16[128,3072]{0,1:T(8,128)(2,1)S(1)}, bf16[128,3072]{0,1:T(8,128)(2,1)S(1)}, u32[]{:S(2)}, u32[]{:S(2)}) %collective-permute-start.5) | collective-permute-done | bytes 786464 | tf_op jit(solution)/shard_map/ppermute | solution.py:43
  303.8 5.7 %collective-permute-start.9 = (bf16[128]{0:T(256)(128)(2,1)S(1)}, bf16[128]{0:T(256)(128)(2,1)S(1)}, u32[]{:S(2)}, u32[]{:S(2)}) collective-permute-start(bf16[128]{0:T(256)(128)(2,1)S(1)} %get-tuple-element.408), channel_id=1, source_target_pairs={{1,0},{2,1},{3,2},{4,3},{5,4},{6,5},{7,6},{8,7},{9,8},{10,9},{11,1... | collective-permute-start | bytes 776 | tf_op jit(solution)/shard_map/ppermute | solution.py:43
  309.5 2.8 reduce_sum.32
  314.8 25.1 %collective-permute-done.6 = bf16[256,3072]{0,1:T(8,128)(2,1)S(1)} collective-permute-done((bf16[256,3072]{0,1:T(8,128)(2,1)S(1)}, bf16[256,3072]{0,1:T(8,128)(2,1)S(1)}, u32[]{:S(2)}, u32[]{:S(2)}) %collective-permute-start.6) | collective-permute-done | bytes 1572896 | tf_op jit(solution)/shard_map/ppermute | solution.py:74
  (162 shorter events, 84.5 us)
Async XLA Ops:
  8.4 15.0 %all-to-all-start = ((s32[32,1,1]{2,1,0:T(1,128)}), s32[32,1,1]{2,1,0:T(1,128)S(1)}, u32[]{:S(2)}, u32[]{:S(2)}) async-start(s32[32,1,1]{2,1,0:T(1,128)} %broadcast_in_dim.73), calls=%async_computation | async-start | bytes 32768 | tf_op jit(solution)/shard_map/all_to_all | solution.py:17
  16.1 79.0 %all-gather.3.cloned.1.call-start = ((), (), s32[]{:S(2)}) async-start(), calls=%async_computation.2 | async-start | bytes 8650752 | tf_op jit(solution)/shard_map/all_gather | solution.py:49
  17.0 9.8 %collective-permute-start.3 = (bf16[128,512]{1,0:T(8,128)(2,1)S(1)}, bf16[128,512]{1,0:T(8,128)(2,1)S(1)}, u32[]{:S(2)}, u32[]{:S(2)}) collective-permute-start(bf16[128,512]{1,0:T(8,128)(2,1)S(1)} %dynamic-slice_bitcast_fusion), channel_id=1, source_target_pairs={{0,1},{1,2},{2,3},{3,4},{4,5},{5,6},{6,7},{7,8},{8,9},{9,10},{10,1... | collective-permute-start | bytes 393224 | tf_op jit(solution)/shard_map/ppermute | solution.py:43
  20.0 8.4 %collective-permute-start.2 = (bf16[128,512]{1,0:T(8,128)(2,1)S(1)}, bf16[128,512]{1,0:T(8,128)(2,1)S(1)}, u32[]{:S(2)}, u32[]{:S(2)}) collective-permute-start(bf16[128,512]{1,0:T(8,128)(2,1)S(1)} %dynamic-slice_bitcast_fusion.1), channel_id=1, source_target_pairs={{0,1},{1,2},{2,3},{3,4},{4,5},{5,6},{6,7},{7,8},{8,9},{9,10},{10,1... | collective-permute-start | bytes 393224 | tf_op jit(solution)/shard_map/ppermute | solution.py:43
  30.0 5.3 %copy-start = (s32[1,256]{1,0:T(1,128)S(1)}, s32[1,256]{1,0:T(1,128)}, u32[]{:S(2)}) copy-start(s32[1,256]{1,0:T(1,128)} %param.20) | copy-start | bytes 3076
  30.1 11.2 %copy-start.1 = (bf16[1,256]{1,0:T(2,128)(2,1)S(1)}, bf16[1,256]{1,0:T(2,128)(2,1)}, u32[]{:S(2)}) copy-start(bf16[1,256]{1,0:T(2,128)(2,1)} %param.19) | copy-start | bytes 1540
  33.4 40.4 %collective-permute-start.4 = (bf16[128,3072]{0,1:T(8,128)(2,1)}, bf16[128,3072]{0,1:T(8,128)(2,1)}, u32[]{:S(2)}, u32[]{:S(2)}) collective-permute-start(bf16[128,3072]{0,1:T(8,128)(2,1)} %bitcast.114), channel_id=1, source_target_pairs={{0,1},{1,2},{2,3},{3,4},{4,5},{5,6},{6,7},{7,8},{8,9},{9,10},{10,1... | collective-permute-start | bytes 2359304 | tf_op jit(solution)/shard_map/ppermute | solution.py:43
  35.4 15.0 %collective-permute-start.1 = (s32[128]{0:T(128)S(1)}, s32[128]{0:T(128)S(1)}, u32[]{:S(2)}, u32[]{:S(2)}) collective-permute-start(s32[128]{0:T(128)S(1)} %fusion.33), channel_id=1, source_target_pairs={{0,1},{1,2},{2,3},{3,4},{4,5},{5,6},{6,7},{7,8},{8,9},{9,10},{10,1... | collective-permute-start | bytes 1544 | tf_op jit(solution)/shard_map/ppermute | solution.py:43
  39.4 112.4 %collective-permute-start.7 = (bf16[128,3072]{0,1:T(8,128)(2,1)}, bf16[128,3072]{0,1:T(8,128)(2,1)}, u32[]{:S(2)}, u32[]{:S(2)}) collective-permute-start(bf16[128,3072]{0,1:T(8,128)(2,1)} %bitcast.33), channel_id=1, source_target_pairs={{0,1},{1,2},{2,3},{3,4},{4,5},{5,6},{6,7},{7,8},{8,9},{9,10},{10,1... | collective-permute-start | bytes 2359304 | tf_op jit(solution)/shard_map/ppermute | solution.py:43
  41.3 112.2 %collective-permute-start = (bf16[128]{0:T(256)(128)(2,1)S(1)}, bf16[128]{0:T(256)(128)(2,1)S(1)}, u32[]{:S(2)}, u32[]{:S(2)}) collective-permute-start(bf16[128]{0:T(256)(128)(2,1)S(1)} %fusion.32), channel_id=1, source_target_pairs={{0,1},{1,2},{2,3},{3,4},{4,5},{5,6},{6,7},{7,8},{8,9},{9,10},{10,1... | collective-permute-start | bytes 776 | tf_op jit(solution)/shard_map/ppermute | solution.py:43
  190.0 119.5 %all-to-all-start.1 = ((bf16[32,128,512]{2,1,0:T(8,128)(2,1)}), bf16[32,128,512]{2,1,0:T(8,128)(2,1)}, u32[]{:S(2)}, u32[]{:S(2)}) async-start(bf16[32,128,512]{2,1,0:T(8,128)(2,1)} %bitcast.110), calls=%async_computation.1 | async-start | bytes 8388608 | tf_op jit(solution)/shard_map/all_to_all | solution.py:68
  244.2 57.7 %collective-permute-start.5 = (bf16[128,3072]{0,1:T(8,128)(2,1)S(1)}, bf16[128,3072]{0,1:T(8,128)(2,1)S(1)}, u32[]{:S(2)}, u32[]{:S(2)}) collective-permute-start(bf16[128,3072]{0,1:T(8,128)(2,1)S(1)} %get-tuple-element.429), channel_id=1, source_target_pairs={{1,0},{2,1},{3,2},{4,3},{5,4},{6,5},{7,6},{8,7},{9,8},{10,9},{11,1... | collective-permute-start | bytes 2359304 | tf_op jit(solution)/shard_map/ppermute | solution.py:43
  302.2 37.8 %collective-permute-start.6 = (bf16[256,3072]{0,1:T(8,128)(2,1)S(1)}, bf16[256,3072]{0,1:T(8,128)(2,1)S(1)}, u32[]{:S(2)}, u32[]{:S(2)}) collective-permute-start(bf16[256,3072]{0,1:T(8,128)(2,1)S(1)} %pad_maximum_fusion), channel_id=1, source_target_pairs={{0,32},{32,64},{64,96},{96,128},{128,160},{160,192},{192,224},{224... | collective-permute-start | bytes 4718600 | tf_op jit(solution)/shard_map/ppermute | solution.py:74
  303.8 10.4 %collective-permute-start.9 = (bf16[128]{0:T(256)(128)(2,1)S(1)}, bf16[128]{0:T(256)(128)(2,1)S(1)}, u32[]{:S(2)}, u32[]{:S(2)}) collective-permute-start(bf16[128]{0:T(256)(128)(2,1)S(1)} %get-tuple-element.408), channel_id=1, source_target_pairs={{1,0},{2,1},{3,2},{4,3},{5,4},{6,5},{7,6},{8,7},{9,8},{10,9},{11,1... | collective-permute-start | bytes 776 | tf_op jit(solution)/shard_map/ppermute | solution.py:43
  312.3 29.3 %collective-permute-start.8 = (bf16[128,512]{1,0:T(8,128)(2,1)S(1)}, bf16[128,512]{1,0:T(8,128)(2,1)S(1)}, u32[]{:S(2)}, u32[]{:S(2)}) collective-permute-start(bf16[128,512]{1,0:T(8,128)(2,1)S(1)} %reduce_sum.32), channel_id=1, source_target_pairs={{1,0},{2,1},{3,2},{4,3},{5,4},{6,5},{7,6},{8,7},{9,8},{10,9},{11,1... | collective-permute-start | bytes 393224 | tf_op jit(solution)/shard_map/ppermute | solution.py:43
Sparse Core Ops, SparseCore 0:
  30.2 64.7 all-gather.2
where the time goes:
time: 351 us; the launch traced here: 349 us
  waiting for transfers between devices  104 us (30%)
  starting transfers between devices  90.6 us (26%)
  local copies, waits for them, and re-layouts  48.6 us (14%)
  other arithmetic  29.5 us (8%)
  blocking collectives  21.7 us (6%)
  loops' own time  21.5 us (6%)
  matrix products  17.3 us (5%)
  between operations  16.4 us (5%)
    ppermute x9, waiting for transfers between devices, passed_along(): return lax.ppermute(block, axis, route)  59.1 us
    all_to_all x1, starting transfers between devices, sent_and_summed(): tiles = lax.all_to_all(in_blocks(x, dim, devices), axis, 0, 0, tiled=True)  54.2 us
    ppermute x9, starting transfers between devices, passed_along(): return lax.ppermute(block, axis, route)  27.1 us
    ppermute x1, waiting for transfers between devices, from_behind(): lax.ppermute(x, axis, [(i, (i + by) % devices) for i in range(devices)])  25.1 us
    all_gather x1, blocking collectives, local(): lax.all_gather(for_sending(place_rows), 'ctx', axis=0, tiled=True)  21.7 us
    all_gather x1, waiting for transfers between devices, sent_together(): out = lax.all_gather(both, axis, axis=dim, tiled=True)  19.5 us
    while x4, local copies, waits for them, and re-layouts, local(): final_state = lax.scan(visit, start_state, stacked)[0]  14.9 us
    another operation x1, loops' own time, local(): final_state = lax.scan(visit, start_state, stacked)[0]  10.5 us
  transfers between devices with their start and end apart: 13, of which 5 were waited for; matrix products, arithmetic and copies ran while one was open for 19% of the time, Pallas kernels for 0%

commit v1 on v0

--- a/solution.py
+++ b/solution.py
@@ -10,6 +10,14 @@
 BLOCK_ROWS = 128
 MAXB = 2
 score_masked_out = -1e30
+
+
+def gather_from_all(shard, axis, dim):
+    size = lax.axis_size(axis)
+    repeats = [size if d == dim else 1 for d in range(shard.ndim)]
+    return lax.all_to_all(
+        jnp.tile(shard, repeats), axis, split_axis=dim, concat_axis=dim, tiled=True
+    )
 
 
 def copy_for_each(x, axis):
@@ -156,7 +164,7 @@
     )
     collected_rows = (
         *sent_together((key_row_block, value_rows), "ctx", 0, 1),
-        lax.all_gather(for_sending(place_rows), "ctx", axis=0, tiled=True).astype(place_rows.dtype),
+        gather_from_all(for_sending(place_rows), "ctx", 0).astype(place_rows.dtype),
     )
     key_complete = collected_rows[0]
     local_row_count = key_complete.shape[0]

time: 351 us -> 353 us (level)
  blocking collectives: 21.7 us -> 0 us
  waiting for transfers between devices: 104 us -> 121 us
  starting transfers between devices: 90.6 us -> 94.6 us
    all_gather x1 -> x0, blocking collectives: 21.7 us -> none  [local(): lax.all_gather(for_sending(place_rows), 'ctx', axis=0, tiled=True)]
    all_gather x1, waiting for transfers between devices: 19.5 us -> 29.3 us  [sent_together(): out = lax.all_gather(both, axis, axis=dim, tiled=True)]
    all_to_all x0 -> x1, starting transfers between devices: none -> 4.97 us  [gather_from_all(): lax.all_to_all(jnp.tile(shard, repeats), axis, split_axis=dim, concat_axi...]
    ppermute x9, waiting for transfers between devices: 59.1 us -> 63.2 us  [passed_along(): return lax.ppermute(block, axis, route)]
  transfers between devices with their start and end apart: 13 -> 14, of which waited for: 5 -> 6; matrix products, arithmetic and copies ran while one was open for 19% -> 19% of each run, Pallas kernels for 0% -> 0%
where the time goes in v1:
time: 353 us; the launch traced here: 351 us
  waiting for transfers between devices  121 us (34%)
  starting transfers between devices  94.6 us (27%)
  local copies, waits for them, and re-layouts  50.2 us (14%)
  other arithmetic  29.5 us (8%)
  loops' own time  22.4 us (6%)
  matrix products  17.3 us (5%)
  between operations  16.4 us (5%)
    ppermute x9, waiting for transfers between devices, passed_along(): return lax.ppermute(block, axis, route)  63.2 us
    all_to_all x1, starting transfers between devices, sent_and_summed(): tiles = lax.all_to_all(in_blocks(x, dim, devices), axis, 0, 0, tiled=True)  54.2 us
    all_gather x1, waiting for transfers between devices, sent_together(): out = lax.all_gather(both, axis, axis=dim, tiled=True)  29.3 us
    ppermute x9, starting transfers between devices, passed_along(): return lax.ppermute(block, axis, route)  26.2 us
    ppermute x1, waiting for transfers between devices, from_behind(): lax.ppermute(x, axis, [(i, (i + by) % devices) for i in range(devices)])  25.2 us
    while x4, local copies, waits for them, and re-layouts, local(): final_state = lax.scan(visit, start_state, stacked)[0]  15 us
    another operation x1, loops' own time, local(): final_state = lax.scan(visit, start_state, stacked)[0]  11 us
    another operation x1, loops' own time, local(): lax.map(lambda member: value_block(member[0], member[1]), (key_portion.re...  10.9 us
  transfers between devices with their start and end apart: 14, of which 6 were waited for; matrix products, arithmetic and copies ran while one was open for 19% of the time, Pallas kernels for 0%

profile of v1, /device:TPU:2, one launch (start us, length us, event | category | flops | bytes accessed | tf_op | source)
XLA Modules:
  0.0 351.3 jit_solution(9729828805899443754)
XLA Ops:
  8.4 7.6 %all-to-all-start = ((s32[32,1,1]{2,1,0:T(1,128)}), s32[32,1,1]{2,1,0:T(1,128)S(1)}, u32[]{:S(2)}, u32[]{:S(2)}) async-start(s32[32,1,1]{2,1,0:T(1,128)} %broadcast_in_dim.73), calls=%async_computation | async-start | bytes 32768 | tf_op jit(solution)/shard_map/all_to_all | solution.py:25
  20.0 3.4 collective-permute-start.2
  35.5 2.8 collective-permute-start.1
  41.4 9.2 %collective-permute-done.1 = s32[128]{0:T(128)S(1)} collective-permute-done((s32[128]{0:T(128)S(1)}, s32[128]{0:T(128)S(1)}, u32[]{:S(2)}, u32[]{:S(2)}) %collective-permute-start.1) | collective-permute-done | bytes 544 | tf_op jit(solution)/shard_map/ppermute | solution.py:51
  51.9 5.0 %all-to-all-start.1 = ((s32[32,128,1]{1,2,0:T(1,128)}), s32[32,128,1]{1,2,0:T(1,128)S(1)}, u32[]{:S(2)}, u32[]{:S(2)}) async-start(s32[32,128,1]{1,2,0:T(1,128)} %all_to_all.17), calls=%async_computation.1 | async-start | bytes 32768 | tf_op jit(solution)/shard_map/all_to_all | solution.py:18
  59.9 3.2 all-to-all-done.1
  65.9 29.3 %all-gather.2.cloned.1.call-done = bf16[4096,1024]{1,0:T(8,128)(2,1)} async-done(((bf16[128,1024]{1,0:T(8,128)(2,1)}), bf16[4096,1024]{1,0:T(8,128)(2,1)}) %all-gather.2.cloned.1.call-update) | async-done | bytes 8388624 | tf_op jit(solution)/shard_map/all_gather | solution.py:57
  95.2 5.8 %fusion.38 = (bf16[4096,512]{1,0:T(8,128)(2,1)}, bf16[4096,512]{1,0:T(8,128)(2,1)}) fusion(bf16[4096,1024]{1,0:T(8,128)(2,1)} %all-gather.2.cloned.1.call-done), kind=kLoop, calls=%fused_computation.78 | loop fusion | bytes 16777216 | tf_op jit(solution)/shard_map/split | solution.py:58
  100.9 6.5 %copy.83 = bf16[8,512,512]{1,2,0:T(8,128)(2,1)} copy(bf16[8,512,512]{2,1,0:T(8,128)(2,1)} %bitcast.106) | data formatting | bytes 8388608 | tf_op jit(solution)/shard_map/while | solution.py:182
  107.4 6.5 %copy.85 = bf16[8,512,512]{1,2,0:T(8,128)(2,1)} copy(bf16[8,512,512]{2,1,0:T(8,128)(2,1)} %bitcast.105) | data formatting | bytes 8388608 | tf_op jit(solution)/shard_map/while | solution.py:182
  114.1 35.1 %while.24 = (s32[]{:T(128)}, f32[4,6,128]{2,1,0:T(8,128)S(1)}, f32[4,6,128]{2,1,0:T(8,128)S(1)}, f32[4,6,128,128]{3,2,1,0:T(8,128)S(1)}, s32[8,512]{1,0:T(8,128)...) while((s32[]{:T(128)}, f32[4,6,128]{2,1,0:T(8,128)S(1)}, ...), condition=%wide.region_7.8_spmd, body=%wide.region_1.7_spmd.sunk | while | flops 823466496 | bytes 26417920 | solution.py:182
  116.1 6.3 %conditional.4 = (f32[4,6,128]{2,1,0:T(8,128)S(1)}, f32[4,6,128]{2,1,0:T(8,128)S(1)}, f32[4,6,128,128]{3,2,1,0:T(8,128)S(1)}) conditional(s32[]{:T(128)} %convert_element_type.71, (s32[1,512]{1,0:T(1,128)S(1)}, s32[128]{0:T(128)S(1)}, bf16[8,512,512]{1,2,0:T(8,128)(2,1)}, s32[]{:T(128)}, bf16[128,4,6,128]{3,0,2,1:T(8,128)(2,1)S(1)}, ...), branch_computations={%region_3.5_spmd, %region_6.6_spmd} | conditional | flops 823465984 | bytes 26389020 | solution.py:154
  124.4 6.3 %conditional.4 = (f32[4,6,128]{2,1,0:T(8,128)S(1)}, f32[4,6,128]{2,1,0:T(8,128)S(1)}, f32[4,6,128,128]{3,2,1,0:T(8,128)S(1)}) conditional(s32[]{:T(128)} %convert_element_type.71, (s32[1,512]{1,0:T(1,128)S(1)}, s32[128]{0:T(128)S(1)}, bf16[8,512,512]{1,2,0:T(8,128)(2,1)}, s32[]{:T(128)}, bf16[128,4,6,128]{3,0,2,1:T(8,128)(2,1)S(1)}, ...), branch_computations={%region_3.5_spmd, %region_6.6_spmd} | conditional | flops 823465984 | bytes 26389020 | solution.py:154
  132.6 6.3 %conditional.4 = (f32[4,6,128]{2,1,0:T(8,128)S(1)}, f32[4,6,128]{2,1,0:T(8,128)S(1)}, f32[4,6,128,128]{3,2,1,0:T(8,128)S(1)}) conditional(s32[]{:T(128)} %convert_element_type.71, (s32[1,512]{1,0:T(1,128)S(1)}, s32[128]{0:T(128)S(1)}, bf16[8,512,512]{1,2,0:T(8,128)(2,1)}, s32[]{:T(128)}, bf16[128,4,6,128]{3,0,2,1:T(8,128)(2,1)S(1)}, ...), branch_computations={%region_3.5_spmd, %region_6.6_spmd} | conditional | flops 823465984 | bytes 26389020 | solution.py:154
  155.7 35.4 %while.25 = (s32[]{:T(128)}, bf16[8,512,512]{2,1,0:T(8,128)(2,1)}, s32[8,512]{1,0:T(8,128)S(1)}, s32[]{:T(128)}, s32[128]{0:T(128)S(1)}, /*index=5*/bf16[8,512,5...) while((s32[]{:T(128)}, bf16[8,512,512]{2,1,0:T(8,128)(2,1)}, ...), condition=%wide.region_12.13_spmd, body=%wide.region_8.12_spmd.sunk | while | flops 811663872 | bytes 5917887 | solution.py:217
  157.7 3.6 %conditional.5 = (bf16[1,512,512]{1,2,0:T(8,128)(2,1)S(1)}) conditional(s32[]{:T(128)} %convert_element_type.72, (s32[1,512]{1,0:T(1,128)S(1)}, s32[128]{0:T(128)S(1)}, bf16[8,512,512]{1,2,0:T(8,128)(2,1)}, s32[]{:T(128)}, bf16[128,4,6,128]{3,0,2,1:T(8,128)(2,1)S(1)}, /*index=5*/f32[4,6,128]{2,1,0:T(8,128)S(1)}, ...), branch_computations={%region_10.10_spmd, %region_11.11_spmd} | conditional | flops 811663360 | bytes 3815948 | solution.py:206
  164.3 3.6 %conditional.5 = (bf16[1,512,512]{1,2,0:T(8,128)(2,1)S(1)}) conditional(s32[]{:T(128)} %convert_element_type.72, (s32[1,512]{1,0:T(1,128)S(1)}, s32[128]{0:T(128)S(1)}, bf16[8,512,512]{1,2,0:T(8,128)(2,1)}, s32[]{:T(128)}, bf16[128,4,6,128]{3,0,2,1:T(8,128)(2,1)S(1)}, /*index=5*/f32[4,6,128]{2,1,0:T(8,128)S(1)}, ...), branch_computations={%region_10.10_spmd, %region_11.11_spmd} | conditional | flops 811663360 | bytes 3815948 | solution.py:206
  170.9 3.6 %conditional.5 = (bf16[1,512,512]{1,2,0:T(8,128)(2,1)S(1)}) conditional(s32[]{:T(128)} %convert_element_type.72, (s32[1,512]{1,0:T(1,128)S(1)}, s32[128]{0:T(128)S(1)}, bf16[8,512,512]{1,2,0:T(8,128)(2,1)}, s32[]{:T(128)}, bf16[128,4,6,128]{3,0,2,1:T(8,128)(2,1)S(1)}, /*index=5*/f32[4,6,128]{2,1,0:T(8,128)S(1)}, ...), branch_computations={%region_10.10_spmd, %region_11.11_spmd} | conditional | flops 811663360 | bytes 3815948 | solution.py:206
  191.1 54.2 %all-to-all-start.2 = ((bf16[32,128,512]{2,1,0:T(8,128)(2,1)}), bf16[32,128,512]{2,1,0:T(8,128)(2,1)}, u32[]{:S(2)}, u32[]{:S(2)}) async-start(bf16[32,128,512]{2,1,0:T(8,128)(2,1)} %bitcast.110), calls=%async_computation.2 | async-start | bytes 8388608 | tf_op jit(solution)/shard_map/all_to_all | solution.py:76
  245.3 4.3 %collective-permute-start.5 = (bf16[128,3072]{0,1:T(8,128)(2,1)S(1)}, bf16[128,3072]{0,1:T(8,128)(2,1)S(1)}, u32[]{:S(2)}, u32[]{:S(2)}) collective-permute-start(bf16[128,3072]{0,1:T(8,128)(2,1)S(1)} %get-tuple-element.429), channel_id=1, source_target_pairs={{1,0},{2,1},{3,2},{4,3},{5,4},{6,5},{7,6},{8,7},{9,8},{10,9},{11,1... | collective-permute-start | bytes 2359304 | tf_op jit(solution)/shard_map/ppermute | solution.py:51
  249.6 53.3 %collective-permute-done.5 = bf16[128,3072]{0,1:T(8,128)(2,1)S(1)} collective-permute-done((bf16[128,3072]{0,1:T(8,128)(2,1)S(1)}, bf16[128,3072]{0,1:T(8,128)(2,1)S(1)}, u32[]{:S(2)}, u32[]{:S(2)}) %collective-permute-start.5) | collective-permute-done | bytes 786464 | tf_op jit(solution)/shard_map/ppermute | solution.py:51
  304.9 5.7 %collective-permute-start.9 = (bf16[128]{0:T(256)(128)(2,1)S(1)}, bf16[128]{0:T(256)(128)(2,1)S(1)}, u32[]{:S(2)}, u32[]{:S(2)}) collective-permute-start(bf16[128]{0:T(256)(128)(2,1)S(1)} %get-tuple-element.408), channel_id=1, source_target_pairs={{1,0},{2,1},{3,2},{4,3},{5,4},{6,5},{7,6},{8,7},{9,8},{10,9},{11,1... | collective-permute-start | bytes 776 | tf_op jit(solution)/shard_map/ppermute | solution.py:51
  310.6 2.8 reduce_sum.32
  315.9 25.2 %collective-permute-done.6 = bf16[256,3072]{0,1:T(8,128)(2,1)} collective-permute-done((bf16[256,3072]{0,1:T(8,128)(2,1)S(1)}, bf16[256,3072]{0,1:T(8,128)(2,1)}, u32[]{:S(2)}, u32[]{:S(2)}) %collective-permute-start.6) | collective-permute-done | bytes 1572896 | tf_op jit(solution)/shard_map/ppermute | solution.py:82
  (164 shorter events, 88.2 us)
Async XLA Ops:
  8.4 15.0 %all-to-all-start = ((s32[32,1,1]{2,1,0:T(1,128)}), s32[32,1,1]{2,1,0:T(1,128)S(1)}, u32[]{:S(2)}, u32[]{:S(2)}) async-start(s32[32,1,1]{2,1,0:T(1,128)} %broadcast_in_dim.73), calls=%async_computation | async-start | bytes 32768 | tf_op jit(solution)/shard_map/all_to_all | solution.py:25
  16.1 79.1 %all-gather.2.cloned.1.call-start = ((), (), s32[]{:S(2)}) async-start(), calls=%async_computation.3 | async-start | bytes 8650752 | tf_op jit(solution)/shard_map/all_gather | solution.py:57
  17.0 9.8 %collective-permute-start.3 = (bf16[128,512]{1,0:T(8,128)(2,1)S(1)}, bf16[128,512]{1,0:T(8,128)(2,1)S(1)}, u32[]{:S(2)}, u32[]{:S(2)}) collective-permute-start(bf16[128,512]{1,0:T(8,128)(2,1)S(1)} %dynamic-slice_bitcast_fusion), channel_id=1, source_target_pairs={{0,1},{1,2},{2,3},{3,4},{4,5},{5,6},{6,7},{7,8},{8,9},{9,10},{10,1... | collective-permute-start | bytes 393224 | tf_op jit(solution)/shard_map/ppermute | solution.py:51
  20.0 8.4 %collective-permute-start.2 = (bf16[128,512]{1,0:T(8,128)(2,1)S(1)}, bf16[128,512]{1,0:T(8,128)(2,1)S(1)}, u32[]{:S(2)}, u32[]{:S(2)}) collective-permute-start(bf16[128,512]{1,0:T(8,128)(2,1)S(1)} %dynamic-slice_bitcast_fusion.1), channel_id=1, source_target_pairs={{0,1},{1,2},{2,3},{3,4},{4,5},{5,6},{6,7},{7,8},{8,9},{9,10},{10,1... | collective-permute-start | bytes 393224 | tf_op jit(solution)/shard_map/ppermute | solution.py:51
  30.0 5.4 %copy-start = (s32[1,256]{1,0:T(1,128)S(1)}, s32[1,256]{1,0:T(1,128)}, u32[]{:S(2)}) copy-start(s32[1,256]{1,0:T(1,128)} %param.20) | copy-start | bytes 3076
  30.1 26.8 %copy-start.1 = (bf16[1,256]{1,0:T(2,128)(2,1)S(1)}, bf16[1,256]{1,0:T(2,128)(2,1)}, u32[]{:S(2)}) copy-start(bf16[1,256]{1,0:T(2,128)(2,1)} %param.19) | copy-start | bytes 1540
  33.5 30.7 %collective-permute-start.4 = (bf16[128,3072]{0,1:T(8,128)(2,1)}, bf16[128,3072]{0,1:T(8,128)(2,1)}, u32[]{:S(2)}, u32[]{:S(2)}) collective-permute-start(bf16[128,3072]{0,1:T(8,128)(2,1)} %bitcast.113), channel_id=1, source_target_pairs={{0,1},{1,2},{2,3},{3,4},{4,5},{5,6},{6,7},{7,8},{8,9},{9,10},{10,1... | collective-permute-start | bytes 2359304 | tf_op jit(solution)/shard_map/ppermute | solution.py:51
  35.5 15.1 %collective-permute-start.1 = (s32[128]{0:T(128)S(1)}, s32[128]{0:T(128)S(1)}, u32[]{:S(2)}, u32[]{:S(2)}) collective-permute-start(s32[128]{0:T(128)S(1)} %fusion.33), channel_id=1, source_target_pairs={{0,1},{1,2},{2,3},{3,4},{4,5},{5,6},{6,7},{7,8},{8,9},{9,10},{10,1... | collective-permute-start | bytes 1544 | tf_op jit(solution)/shard_map/ppermute | solution.py:51
  39.5 112.9 %collective-permute-start.7 = (bf16[128,3072]{0,1:T(8,128)(2,1)}, bf16[128,3072]{0,1:T(8,128)(2,1)}, u32[]{:S(2)}, u32[]{:S(2)}) collective-permute-start(bf16[128,3072]{0,1:T(8,128)(2,1)} %bitcast.32), channel_id=1, source_target_pairs={{0,1},{1,2},{2,3},{3,4},{4,5},{5,6},{6,7},{7,8},{8,9},{9,10},{10,1... | collective-permute-start | bytes 2359304 | tf_op jit(solution)/shard_map/ppermute | solution.py:51
  51.9 11.2 %all-to-all-start.1 = ((s32[32,128,1]{1,2,0:T(1,128)}), s32[32,128,1]{1,2,0:T(1,128)S(1)}, u32[]{:S(2)}, u32[]{:S(2)}) async-start(s32[32,128,1]{1,2,0:T(1,128)} %all_to_all.17), calls=%async_computation.1 | async-start | bytes 32768 | tf_op jit(solution)/shard_map/all_to_all | solution.py:18
  56.9 97.2 %collective-permute-start = (bf16[128]{0:T(256)(128)(2,1)S(1)}, bf16[128]{0:T(256)(128)(2,1)S(1)}, u32[]{:S(2)}, u32[]{:S(2)}) collective-permute-start(bf16[128]{0:T(256)(128)(2,1)S(1)} %fusion.32), channel_id=1, source_target_pairs={{0,1},{1,2},{2,3},{3,4},{4,5},{5,6},{6,7},{7,8},{8,9},{9,10},{10,1... | collective-permute-start | bytes 776 | tf_op jit(solution)/shard_map/ppermute | solution.py:51
  191.1 119.5 %all-to-all-start.2 = ((bf16[32,128,512]{2,1,0:T(8,128)(2,1)}), bf16[32,128,512]{2,1,0:T(8,128)(2,1)}, u32[]{:S(2)}, u32[]{:S(2)}) async-start(bf16[32,128,512]{2,1,0:T(8,128)(2,1)} %bitcast.110), calls=%async_computation.2 | async-start | bytes 8388608 | tf_op jit(solution)/shard_map/all_to_all | solution.py:76
  245.3 57.7 %collective-permute-start.5 = (bf16[128,3072]{0,1:T(8,128)(2,1)S(1)}, bf16[128,3072]{0,1:T(8,128)(2,1)S(1)}, u32[]{:S(2)}, u32[]{:S(2)}) collective-permute-start(bf16[128,3072]{0,1:T(8,128)(2,1)S(1)} %get-tuple-element.429), channel_id=1, source_target_pairs={{1,0},{2,1},{3,2},{4,3},{5,4},{6,5},{7,6},{8,7},{9,8},{10,9},{11,1... | collective-permute-start | bytes 2359304 | tf_op jit(solution)/shard_map/ppermute | solution.py:51
  303.2 37.9 %collective-permute-start.6 = (bf16[256,3072]{0,1:T(8,128)(2,1)S(1)}, bf16[256,3072]{0,1:T(8,128)(2,1)}, u32[]{:S(2)}, u32[]{:S(2)}) collective-permute-start(bf16[256,3072]{0,1:T(8,128)(2,1)S(1)} %pad_maximum_fusion), channel_id=1, source_target_pairs={{0,32},{32,64},{64,96},{96,128},{128,160},{160,192},{192,224},{224... | collective-permute-start | bytes 4718600 | tf_op jit(solution)/shard_map/ppermute | solution.py:82
  304.9 10.4 %collective-permute-start.9 = (bf16[128]{0:T(256)(128)(2,1)S(1)}, bf16[128]{0:T(256)(128)(2,1)S(1)}, u32[]{:S(2)}, u32[]{:S(2)}) collective-permute-start(bf16[128]{0:T(256)(128)(2,1)S(1)} %get-tuple-element.408), channel_id=1, source_target_pairs={{1,0},{2,1},{3,2},{4,3},{5,4},{6,5},{7,6},{8,7},{9,8},{10,9},{11,1... | collective-permute-start | bytes 776 | tf_op jit(solution)/shard_map/ppermute | solution.py:51
  313.4 30.3 %collective-permute-start.8 = (bf16[128,512]{1,0:T(8,128)(2,1)S(1)}, bf16[128,512]{1,0:T(8,128)(2,1)S(1)}, u32[]{:S(2)}, u32[]{:S(2)}) collective-permute-start(bf16[128,512]{1,0:T(8,128)(2,1)S(1)} %reduce_sum.32), channel_id=1, source_target_pairs={{1,0},{2,1},{3,2},{4,3},{5,4},{6,5},{7,6},{8,7},{9,8},{10,9},{11,1... | collective-permute-start | bytes 393224 | tf_op jit(solution)/shard_map/ppermute | solution.py:51
Sparse Core Ops, SparseCore 0:
  30.2 64.9 all-gather.1
